TPU v7x, 32 devices: a whole 2x2x4 slice. The times are simulated.
32 devices in a mesh: dp: 8 (over z, x), col: 4 (over y, core).
Axes of the slice: x: 2, y: 2, z: 4, core: 2. Of those that a mesh axis runs over, the one named last changes fastest.
Arguments:
- tokens: bfloat16 [2048, 5120], P('dp', 'col'), may hold values from -72 to 72
- query_weight: bfloat16 [5120, 5120], P('dp', 'col'), may hold values from -0.078125 to 0.078125
- key_weight: bfloat16 [5120, 5120], P('dp', 'col'), may hold values from -0.078125 to 0.078125
- old_maps: bfloat16 [960, 8, 256, 256], P(None, 'dp', 'col'), may hold values from 9.9658966e-05 to 0.5
- pair_weight: bfloat16 [1000, 128], replicated, may hold values from -0.75 to 0.75
- pair_bias: float32 [128], replicated, may hold values from -1.5 to 1.5
- norm_gain: float32 [128], replicated, may hold values from 0.25 to 1.75
- norm_bias: float32 [128], replicated, may hold values from -1.5 to 1.5
- hidden_weight: bfloat16 [128, 512], replicated, may hold values from -0.5 to 0.5
- hidden_bias: float32 [512], replicated, may hold values from -1.5 to 1.5
- out_weight: bfloat16 [512, 128], replicated, may hold values from -0.25 to 0.25
- out_bias: float32 [128], replicated, may hold values from -1.5 to 1.5
- chain_starts: int32 [8, 8], P('dp'), may hold values from 0 to 244, as said below
- chain_lengths: int32 [8, 8], P('dp'), may hold values from 12 to 172
- chain_groups: int32 [8, 8], P('dp'), may hold values from 0 to 7, as said below
- tile_owner: int32 [8, 4, 8], P('dp', 'col'), may hold values from -1 to 7, as said below
Outputs:
- pair_tiles: bfloat16 [8, 8, 4, 2048, 128], P('dp', None, 'col')
Inputs may be any that keep to these rules, and one draw needn't show every extreme that they name: `chain_starts`: in each bin the chains do not intersect, lie in increasing order and end exactly at token 256; between two chains at most 4 tokens belong to no chain. `chain_groups`: complex numbers start at 0 in each bin and never fall along the chains; only tokens of one complex attend to each other. `tile_owner`: A tile's owner is -1 exactly when the tile holds no pair of two tokens of one complex. Within one bin and key block, tiles have distinct owners; for each key block one owner receives a tile from every bin, so an owner receives at most 8 tiles of a key block.
All inputs are finite; a program needn't handle non-finite values.
Results may differ from a plain program's by a relative error of at most 0.012.
Values may be sent and summed in bfloat16 or wider, within the bound.
A program may use at most 192 MiB of HBM per device.

v0:
```python
import math

import jax
import jax.numpy as jnp
from jax import lax
from jax.sharding import PartitionSpec as P

HEAD = 128


def chain_tokens(starts, lengths, groups, token_count):
    places = jnp.arange(token_count, dtype=jnp.int32)
    member = (places[:, None] >= starts[None, :]) & (places[:, None] < (starts + lengths)[None, :])
    inside = jnp.any(member, axis=1)
    group_ids = jnp.sum(jnp.where(member, groups[None, :], 0), axis=1)
    offset = jnp.sum(jnp.where(member, places[:, None] - starts[None, :], 0), axis=1)
    return (inside, group_ids, offset.astype(jnp.float32))


def rotate(values, offset):
    half_width = values.shape[-1] // 2
    frequency = jnp.exp(
        jnp.arange(half_width).astype(jnp.float32) * (-2.0 * math.log(10000.0) / values.shape[-1])
    )
    angles = offset[:, None] * frequency[None, :]
    cosine = jnp.cos(angles)[:, None, :]
    sine_table = jnp.sin(angles)[:, None, :]
    former = values[..., :half_width]
    latter = values[..., half_width:]
    return jnp.concatenate(
        [former * cosine - latter * sine_table, latter * cosine + former * sine_table], axis=-1
    )


def head_maps(queries, key_rows, allowed):
    scores = jnp.einsum(
        "jhd,ihd->hji", key_rows, queries, preferred_element_type=jnp.float32
    ) / math.sqrt(queries.shape[-1])
    masked = jnp.where(allowed[None], scores, -jnp.inf)
    largest = jnp.max(masked, axis=1, keepdims=True)
    powers = jnp.exp(masked - largest)
    return (powers / jnp.sum(powers, axis=1, keepdims=True)).astype(jnp.bfloat16)


def refine(
    pair_rows, valid, norm_gain, norm_bias, hidden_weight, hidden_bias, out_weight, out_bias
):
    values = pair_rows.astype(jnp.float32)
    average = jnp.mean(values, axis=-1, keepdims=True)
    centred = values - average
    spread = jnp.mean(centred * centred, axis=-1, keepdims=True)
    normed = (centred * lax.rsqrt(spread + 1e-05) * norm_gain + norm_bias).astype(jnp.bfloat16)
    hidden = jnp.maximum(
        jnp.dot(normed, hidden_weight, preferred_element_type=jnp.float32) + hidden_bias, 0.0
    ).astype(jnp.bfloat16)
    update = jnp.dot(hidden, out_weight, preferred_element_type=jnp.float32) + out_bias
    return (valid[:, None] * (values + update)).astype(jnp.bfloat16)


def body(
    tokens,
    query_weight,
    key_weight,
    old_maps,
    pair_weight,
    pair_bias,
    norm_gain,
    norm_bias,
    hidden_weight,
    hidden_bias,
    out_weight,
    out_bias,
    chain_starts,
    chain_lengths,
    chain_groups,
    tile_owner,
):
    column_count = lax.axis_size("col")
    row_count = lax.axis_size("dp")
    gathered = lax.all_gather(tokens, "col", axis=1, tiled=True)
    bin_tokens = gathered.shape[0]
    head_cols = query_weight.shape[1]
    query_sum = jnp.dot(
        gathered,
        lax.all_gather(query_weight, "dp", axis=0, tiled=True),
        preferred_element_type=jnp.float32,
    )
    key_sum = jnp.dot(
        gathered,
        lax.all_gather(key_weight, "dp", axis=0, tiled=True),
        preferred_element_type=jnp.float32,
    )
    heads_here = head_cols // HEAD
    inside, group_ids, offset = chain_tokens(
        chain_starts[0], chain_lengths[0], chain_groups[0], bin_tokens
    )
    queries = rotate(query_sum.reshape(bin_tokens, heads_here, HEAD), offset).astype(jnp.bfloat16)
    key_rows = rotate(key_sum.reshape(bin_tokens, heads_here, HEAD), offset).astype(jnp.bfloat16)
    same_group = inside[:, None] & inside[None, :] & (group_ids[:, None] == group_ids[None, :])
    allowed = same_group | jnp.eye(bin_tokens, dtype=bool)
    prob_maps = head_maps(queries, key_rows, allowed)
    spread_maps = lax.all_to_all(prob_maps, "col", split_axis=1, concat_axis=0, tiled=True)
    block_width = bin_tokens // column_count
    start_key = lax.axis_index("col") * block_width
    key_group = lax.dynamic_slice_in_dim(same_group, start_key, block_width, 0)
    old_channels = old_maps.shape[0]
    earlier = old_maps.reshape(old_channels, -1)
    pair_rows = jnp.dot(earlier.T, pair_weight[:old_channels], preferred_element_type=jnp.float32)
    pair_rows = pair_rows + jnp.dot(
        spread_maps.reshape(spread_maps.shape[0], -1).T,
        pair_weight[old_channels:],
        preferred_element_type=jnp.float32,
    )
    pair_rows = (pair_rows + pair_bias).astype(jnp.bfloat16)
    owners = tile_owner[0, 0]
    row_tiles = owners.shape[0]
    tile_rows = bin_tokens // row_tiles
    pair_width = pair_rows.shape[1]
    select = (owners[None, :] == jnp.arange(row_count, dtype=jnp.int32)[:, None]).astype(
        jnp.bfloat16
    )
    refined = refine(
        pair_rows,
        key_group.reshape(-1).astype(jnp.float32),
        norm_gain,
        norm_bias,
        hidden_weight,
        hidden_bias,
        out_weight,
        out_bias,
    )
    outgoing = jnp.einsum(
        "dr,jrip->djip",
        select,
        refined.reshape(block_width, row_tiles, tile_rows, pair_width),
        preferred_element_type=jnp.float32,
    )
    outgoing = outgoing.astype(jnp.bfloat16).reshape(row_count, block_width * tile_rows, pair_width)
    arrived = lax.all_to_all(outgoing, "dp", split_axis=0, concat_axis=0, tiled=True)
    return arrived.reshape(1, row_count, 1, arrived.shape[1], pair_width)


def solution(mesh):
    in_specs = (
        P("dp", "col"),
        P("dp", "col"),
        P("dp", "col"),
        P(None, "dp", "col", None),
        P(),
        P(),
        P(),
        P(),
        P(),
        P(),
        P(),
        P(),
        P("dp", None),
        P("dp", None),
        P("dp", None),
        P("dp", "col", None),
    )
    out_specs = P("dp", None, "col", None, None)
    return jax.shard_map(body, mesh=mesh, in_specs=in_specs, out_specs=out_specs, check_vma=False)
```

profile of v0, /device:TPU:0, one launch (start us, length us, event | category | flops | bytes accessed | tf_op | source)
XLA Modules:
  0.0 593.0 jit_solution(16475286933016645397)
XLA Ops:
  6.5 0.7 all-gather.4.cloned.1.call-update
  7.3 0.0 all-gather.8.cloned.1.call-start
  7.3 0.7 all-gather.8.cloned.1.call-update
  8.0 0.0 all-gather.6.cloned.1.call-start
  8.1 0.7 all-gather.6.cloned.1.call-update
  8.8 29.2 %copy.60 = bf16[120,8,64,256]{3,1,2,0:T(8,128)(2,1)} copy(bf16[120,8,64,256]{3,2,1,0:T(8,128)(2,1)} %bitcast.35) | data formatting | bytes 62914560
  38.0 0.1 select_reduce_fusion
  38.1 0.1 fusion.44
  38.2 0.8 compare_and_fusion
  39.0 0.7 copy.59
  39.7 1.2 multiply_cosine_fusion
  40.9 181.0 %all-gather.8.cloned.1.call-done = bf16[5120,1280]{1,0:T(8,128)(2,1)} async-done(((bf16[640,1280]{1,0:T(8,128)(2,1)}), bf16[5120,1280]{1,0:T(8,128)(2,1)}) %all-gather.8.cloned.1.call-update) | async-done | bytes 13107216 | tf_op jit(solution)/shard_map/all_gather | solution.py:85
  221.9 9.0 %fusion.67 = f32[256,1280]{0,1:T(8,128)S(1)} fusion(bf16[256,5120]{1,0:T(8,128)(2,1)} %all-gather.4.cloned.1.call-done, bf16[5120,1280]{1,0:T(8,128)(2,1)} %all-gather.8.cloned.1.call-done), kind=kOutput, calls=%fused_computation.69 | convolution fusion | flops 3355443200 | bytes 17039360 | tf_op jit(solution)/shard_map/dot_general | solution.py:83
  230.9 0.1 fusion.58
  231.0 0.4 copy.58
  231.4 0.4 copy.57
  231.8 173.0 %all-gather.6.cloned.1.call-done = bf16[5120,1280]{1,0:T(8,128)(2,1)} async-done(((bf16[640,1280]{1,0:T(8,128)(2,1)}), bf16[5120,1280]{1,0:T(8,128)(2,1)}) %all-gather.6.cloned.1.call-update) | async-done | bytes 13107216 | tf_op jit(solution)/shard_map/all_gather | solution.py:90
  404.8 9.1 %fusion.66 = f32[256,1280]{0,1:T(8,128)S(1)} fusion(bf16[256,5120]{1,0:T(8,128)(2,1)} %all-gather.4.cloned.1.call-done, bf16[5120,1280]{1,0:T(8,128)(2,1)} %all-gather.6.cloned.1.call-done), kind=kOutput, calls=%fused_computation.68 | convolution fusion | flops 3355443200 | bytes 17039360 | tf_op jit(solution)/shard_map/dot_general | solution.py:88
  413.9 1.0 fusion.59
  414.9 2.5 copy.55
  417.5 1.5 copy.56
  419.0 3.5 subtract_convert_fusion
  422.5 2.9 fusion.60
  425.4 0.2 divide_convert_fusion
  425.7 0.0 copy-start.2
  425.7 2.1 copy.48
  427.8 3.6 all-to-all-start
  431.5 16.7 %fusion.40 = f32[16384,128]{1,0:T(8,128)} fusion(bf16[960,16384]{1,0:T(8,128)(2,1)} %bitcast.34, bf16[1000,128]{1,0:T(8,128)(2,1)S(1)} %copy-done.2), kind=kOutput, calls=%fused_computation.40 | convolution fusion | flops 4026531840 | bytes 40091648 | tf_op jit(solution)/shard_map/dot_general | solution.py:108
  448.1 8.9 %all-to-all-done = bf16[10,256,256]{2,0,1:T(8,128)(2,1)S(1)} async-done(((bf16[10,256,256]{2,0,1:T(8,128)(2,1)}), bf16[10,256,256]{2,0,1:T(8,128)(2,1)S(1)}, u32[]{:S(2)}, u32[]{:S(2)}) %all-to-all-start) | async-done | bytes 1310752 | tf_op jit(solution)/shard_map/all_to_all | solution.py:102
  457.1 0.5 copy.49
  457.6 0.8 copy.61
  458.3 6.8 %fusion.65 = (f32[16384]{0:T(1024)S(1)}, f32[16384,128]{1,0:T(8,128)S(1)}) fusion(f32[128]{0:T(128)S(1)} %copy-done.4, f32[16384,128]{1,0:T(8,128)} %fusion.40, bf16[40,16384]{1,0:T(8,128)(2,1)S(1)} %bitcast.39, bf16[1000,128]{1,0:T(8,128)(2,1)S(1)} %copy-done.2), kind=kOutput, calls=%fused_computation.67 | convolution fusion | flops 178241536 | bytes 18164224 | tf_op jit(solution)/shard_map/dot_general | solution.py:109
  465.2 0.0 copy-start.8
  465.2 0.0 copy-start.9
  465.2 0.0 copy-start.11
  465.3 0.0 copy-start.12
  465.3 0.0 copy-start.13
  465.3 4.9 multiply_reduce_fusion
  470.2 0.0 copy-done
  470.2 0.0 copy-done.3
  470.2 0.0 copy-done.8
  470.2 0.0 copy-done.9
  470.3 0.0 copy-start.5
  470.3 14.3 %fusion.4 = bf16[16384,128]{1,0:T(8,128)(2,1)} fusion(f32[16384,128]{1,0:T(8,128)} %copy-done.1, bf16[512,128]{1,0:T(8,128)(2,1)S(1)} %copy-done, bf16[128,512]{1,0:T(8,128)(2,1)S(1)} %copy-done.8, f32[512]{0:T(512)S(1)} %copy-done.9, f32[128]{0:T(128)S(1)} %copy-done.11, f32[128]{0:T(128)S(1)} %copy-done.12, f32[128]{0:T(128)S(1)} %copy-done.13, ...), kind=kOutput, calls=%fused_computation.7 | convolution fusion | flops 4339007488 | bytes 13045248 | tf_op jit(solution)/shard_map/dot_general | solution.py:56
  484.6 3.7 fusion.17
  488.3 0.5 copy.51
  488.8 95.6 %all_to_all.20 = bf16[8,2048,128]{2,1,0:T(8,128)(2,1)S(1)} all-to-all(bf16[8,2048,128]{2,1,0:T(8,128)(2,1)S(1)} %copy.51), channel_id=1, replica_groups=mesh['dp'=8,'col'=4] {'dp'}, dimensions={0} | all-to-all | bytes 8388608 | tf_op jit(solution)/shard_map/all_to_all | solution.py:139
  584.5 2.0 copy.67
  (25 shorter events, 0.1 us)
Async XLA Ops:
  6.5 463.7 %copy-start = (bf16[512,128]{1,0:T(8,128)(2,1)S(1)}, bf16[512,128]{1,0:T(8,128)(2,1)}, u32[]{:S(2)}) copy-start(bf16[512,128]{1,0:T(8,128)(2,1)} %param.26) | copy-start | bytes 393220
  6.5 34.3 %all-gather.4.cloned.1.call-start = ((), (), s32[]{:S(2)}) async-start(), calls=%async_computation.2 | async-start | bytes 3276800 | tf_op jit(solution)/shard_map/all_gather | solution.py:80
  7.3 214.6 %all-gather.8.cloned.1.call-start = ((), (), s32[]{:S(2)}) async-start(), calls=%async_computation.4 | async-start | bytes 14745600 | tf_op jit(solution)/shard_map/all_gather | solution.py:85
  8.0 396.8 %all-gather.6.cloned.1.call-start = ((), (), s32[]{:S(2)}) async-start(), calls=%async_computation.3 | async-start | bytes 14745600 | tf_op jit(solution)/shard_map/all_gather | solution.py:90
  8.7 29.3 %copy-start.7 = (s32[1,8]{1,0:T(1,128)S(1)}, s32[1,8]{1,0:T(1,128)}, u32[]{:S(2)}) copy-start(s32[1,8]{1,0:T(1,128)} %param.28) | copy-start | bytes 100
  8.8 29.2 %copy-start.10 = (s32[1,8]{1,0:T(1,128)S(1)}, s32[1,8]{1,0:T(1,128)}, u32[]{:S(2)}) copy-start(s32[1,8]{1,0:T(1,128)} %param.29) | copy-start | bytes 100
  8.8 29.3 %copy-start.6 = (s32[1,8]{1,0:T(1,128)S(1)}, s32[1,8]{1,0:T(1,128)}, u32[]{:S(2)}) copy-start(s32[1,8]{1,0:T(1,128)} %param.30) | copy-start | bytes 100
  425.7 5.8 copy-start.2
  427.8 29.2 %all-to-all-start = ((bf16[10,256,256]{2,0,1:T(8,128)(2,1)}), bf16[10,256,256]{2,0,1:T(8,128)(2,1)S(1)}, u32[]{:S(2)}, u32[]{:S(2)}) async-start(bf16[10,256,256]{2,0,1:T(8,128)(2,1)} %copy.48), calls=%async_computation | async-start | bytes 4194304 | tf_op jit(solution)/shard_map/all_to_all | solution.py:102
  448.1 10.2 %copy-start.4 = (f32[128]{0:T(128)S(1)}, f32[128]{0:T(128)}, u32[]{:S(2)}) copy-start(f32[128]{0:T(128)} %param.21) | copy-start | bytes 1540
  465.2 5.0 copy-start.1
  465.2 5.0 copy-start.3
  465.2 5.0 copy-start.8
  465.2 5.0 copy-start.9
  465.2 5.0 copy-start.11
  465.3 5.0 copy-start.12
  465.3 5.0 copy-start.13
  470.3 14.3 %copy-start.5 = (s32[1,1,8]{2,1,0:T(1,128)S(1)}, s32[1,1,8]{2,1,0:T(1,128)}, u32[]{:S(2)}) copy-start(s32[1,1,8]{2,1,0:T(1,128)} %param.31) | copy-start | bytes 100
Sparse Core Ops, SparseCore 0:
  8.9 28.2 all-gather.3
  39.4 182.4 all-gather.7
  224.1 180.6 all-gather.5
where the time goes:
time: 593 us
  waiting for transfers between devices  365 us (62%)
  blocking collectives  95.6 us (16%)
  matrix products  62.5 us (11%)
  local copies, waits for them, and re-layouts  41.8 us (7%)
  between operations  13.4 us (2%)
  other arithmetic  10.8 us (2%)
    all_gather x1, waiting for transfers between devices, body(): lax.all_gather(query_weight, 'dp', axis=0, tiled=True)  181 us
    all_gather x1, waiting for transfers between devices, body(): lax.all_gather(key_weight, 'dp', axis=0, tiled=True)  173 us
    all_to_all x1, blocking collectives, body(): lax.all_to_all(outgoing, 'dp', split_axis=0, concat_axis=0, tiled=True)  95.6 us
    unnamed x36, local copies, waits for them, and re-layouts  37.6 us
    dot_general x1, matrix products, body(): jnp.dot(earlier.T, pair_weight[:old_channels], preferred_element_type=jnp...  16.7 us
    dot_general x1, matrix products, refine(): jnp.dot(hidden, out_weight, preferred_element_type=jnp.float32) + out_bias  14.3 us
  transfers between devices with their start and end apart: 4, of which 3 were waited for; matrix products, arithmetic and copies ran while one was open for 10% of the time, Pallas kernels for 0%

commit v1 on v0

--- a/solution.py
+++ b/solution.py
@@ -77,19 +77,26 @@
 ):
     column_count = lax.axis_size("col")
     row_count = lax.axis_size("dp")
-    gathered = lax.all_gather(tokens, "col", axis=1, tiled=True)
-    bin_tokens = gathered.shape[0]
+    bin_tokens = tokens.shape[0]
     head_cols = query_weight.shape[1]
-    query_sum = jnp.dot(
-        gathered,
-        lax.all_gather(query_weight, "dp", axis=0, tiled=True),
-        preferred_element_type=jnp.float32,
+    by_rows = lax.all_to_all(tokens, "col", split_axis=0, concat_axis=1, tiled=True)
+    share = by_rows.shape[0]
+    depth = query_weight.shape[0]
+    by_columns = lax.all_to_all(
+        by_rows.reshape(share, row_count, depth), "dp", split_axis=1, concat_axis=1, tiled=True
     )
-    key_sum = jnp.dot(
-        gathered,
-        lax.all_gather(key_weight, "dp", axis=0, tiled=True),
-        preferred_element_type=jnp.float32,
-    )
+    columns = lax.all_gather(
+        by_columns.reshape(share, row_count, depth).transpose(1, 0, 2), "col", axis=1, tiled=True
+    ).reshape(row_count * bin_tokens, depth)
+
+    def project(weight):
+        partial = jnp.dot(columns, weight, preferred_element_type=jnp.float32)
+        return lax.psum_scatter(
+            partial.astype(jnp.bfloat16), "dp", scatter_dimension=0, tiled=True
+        ).astype(jnp.float32)
+
+    query_sum = project(query_weight)
+    key_sum = project(key_weight)
     heads_here = head_cols // HEAD
     inside, group_ids, offset = chain_tokens(
         chain_starts[0], chain_lengths[0], chain_groups[0], bin_tokens

time: 593 us -> 483 us (0.81)
  waiting for transfers between devices: 365 us -> 198 us
  blocking collectives: 95.6 us -> 135 us
  local copies, waits for them, and re-layouts: 41.8 us -> 58.3 us
    all_gather x3 -> x1, waiting for transfers between devices: 354 us -> 23.6 us  [body(): lax.all_gather(by_columns.reshape(share, row_count, depth).transpose(1, 0...]
    reduce_scatter x0 -> x2, waiting for transfers between devices: none -> 165 us  [project(): lax.psum_scatter(partial.astype(jnp.bfloat16), 'dp', scatter_dimension=0,...]
    all_to_all x0 -> x2, blocking collectives: none -> 38.2 us  [the longest x1 23.6 us: body(): lax.all_to_all(by_rows.reshape(share, row_count, depth), 'dp', split_axis...]
    unnamed x36 -> x42, local copies, waits for them, and re-layouts: 37.6 us -> 42.4 us
  transfers between devices with their start and end apart: 4 -> 4, of which waited for: 3 -> 4; matrix products, arithmetic and copies ran while one was open for 10% -> 12% of each run, Pallas kernels for 0% -> 0%
where the time goes in v1:
time: 483 us; the launch traced here: 482 us
  waiting for transfers between devices  198 us (41%)
  blocking collectives  135 us (28%)
  matrix products  60.4 us (13%)
  local copies, waits for them, and re-layouts  58.3 us (12%)
  between operations  13.5 us (3%)
  other arithmetic  11.6 us (2%)
  starting transfers between devices  5.11 us (1%)
    reduce_scatter x2, waiting for transfers between devices, project(): lax.psum_scatter(partial.astype(jnp.bfloat16), 'dp', scatter_dimension=0,...  165 us
    all_to_all x1, blocking collectives, body(): lax.all_to_all(outgoing, 'dp', split_axis=0, concat_axis=0, tiled=True)  97.1 us
    unnamed x42, local copies, waits for them, and re-layouts  42.4 us
    all_gather x1, waiting for transfers between devices, body(): lax.all_gather(by_columns.reshape(share, row_count, depth).transpose(1, 0...  23.6 us
    all_to_all x1, blocking collectives, body(): lax.all_to_all(by_rows.reshape(share, row_count, depth), 'dp', split_axis...  23.6 us
    dot_general x1, matrix products, body(): jnp.dot(earlier.T, pair_weight[:old_channels], preferred_element_type=jnp...  16.7 us
    all_to_all x1, blocking collectives, body(): lax.all_to_all(tokens, 'col', split_axis=0, concat_axis=1, tiled=True)  14.6 us
    dot_general x1, matrix products, refine(): jnp.dot(hidden, out_weight, preferred_element_type=jnp.float32) + out_bias  14.4 us
  transfers between devices with their start and end apart: 4, of which 4 were waited for; matrix products, arithmetic and copies ran while one was open for 12% of the time, Pallas kernels for 0%

profile of v1, /device:TPU:0, one launch (start us, length us, event | category | flops | bytes accessed | tf_op | source)
XLA Modules:
  0.0 481.9 jit_solution(8899087800928218188)
XLA Ops:
  6.5 14.6 %all_to_all.41 = bf16[4,64,1280]{2,1,0:T(8,128)(2,1)S(1)} all-to-all(bf16[4,64,1280]{2,1,0:T(8,128)(2,1)} %bitcast.51), channel_id=1, replica_groups=mesh['dp'=8,'col'=4] {'col'}, dimensions={0} | all-to-all | bytes 1310720 | tf_op jit(solution)/shard_map/all_to_all | solution.py:82
  21.2 0.5 copy.48
  21.7 0.2 reshape.182
  21.8 0.1 copy.49
  21.9 23.6 %all_to_all.42 = bf16[64,8,640]{2,0,1:T(8,128)(2,1)S(1)} all-to-all(bf16[64,8,640]{2,0,1:T(8,128)(2,1)S(1)} %copy.49), channel_id=1, replica_groups=mesh['dp'=8,'col'=4] {'dp'}, dimensions={1} | all-to-all | bytes 1310720 | tf_op jit(solution)/shard_map/all_to_all | solution.py:85
  45.5 1.2 copy.50
  46.7 0.0 all-gather.2.cloned.1.call-update
  46.8 0.0 reduce-scatter.5.cloned.1.call-start
  46.8 23.6 %all-gather.2.cloned.1.call-done = bf16[8,256,640]{2,0,1:T(8,128)(2,1)} async-done(((bf16[8,64,640]{2,0,1:T(8,128)(2,1)}), bf16[8,256,640]{2,0,1:T(8,128)(2,1)}) %all-gather.2.cloned.1.call-update) | async-done | bytes 2621456 | tf_op jit(solution)/shard_map/all_gather | solution.py:88
  70.5 2.1 copy.51
  72.5 1.5 copy-done.3
  74.0 5.9 %convolution_convert_fusion = bf16[2048,1280]{1,0:T(8,128)(2,1)} fusion(bf16[2048,640]{1,0:T(8,128)(2,1)S(1)} %bitcast.47, bf16[640,1280]{1,0:T(8,128)(2,1)S(1)} %copy-done), kind=kOutput, calls=%fused_computation.12 | convolution fusion | flops 3358064640 | bytes 9502720 | tf_op jit(solution)/shard_map/dot_general | solution.py:93
  80.0 0.2 reduce-scatter.3.cloned.1.call-start
  80.2 1.2 copy-done.9
  81.4 8.3 %convolution_convert_fusion.1 = bf16[2048,1280]{1,0:T(8,128)(2,1)} fusion(bf16[2048,640]{1,0:T(8,128)(2,1)} %bitcast.48, bf16[640,1280]{1,0:T(8,128)(2,1)S(1)} %copy-done.9), kind=kOutput, calls=%fused_computation.13 | convolution fusion | flops 3358064640 | bytes 9502720 | tf_op jit(solution)/shard_map/dot_general | solution.py:93
  89.6 0.0 reduce-scatter.3.cloned.1.call-update
  89.7 29.2 %copy.68 = bf16[120,8,64,256]{3,1,2,0:T(8,128)(2,1)} copy(bf16[120,8,64,256]{3,2,1,0:T(8,128)(2,1)} %bitcast.39) | data formatting | bytes 62914560
  119.0 0.1 select_reduce_fusion
  119.1 0.1 fusion.44
  119.2 0.1 compare_and_fusion
  119.4 0.5 multiply_cosine_fusion
  119.9 63.2 %reduce-scatter.5.cloned.1.call-done = bf16[256,1280]{1,0:T(8,128)(2,1)} async-done(((bf16[2048,1280]{1,0:T(8,128)(2,1)}), bf16[256,1280]{1,0:T(8,128)(2,1)}) %reduce-scatter.5.cloned.1.call-update) | async-done | bytes 655376 | tf_op jit(solution)/shard_map/reduce_scatter | solution.py:94
  183.1 1.3 copy.55
  184.5 1.0 fusion.58
  185.4 0.4 copy.66
  185.8 1.5 copy.65
  187.3 102.1 %reduce-scatter.3.cloned.1.call-done = bf16[256,1280]{1,0:T(8,128)(2,1)} async-done(((bf16[2048,1280]{1,0:T(8,128)(2,1)}), bf16[256,1280]{1,0:T(8,128)(2,1)}) %reduce-scatter.3.cloned.1.call-update) | async-done | bytes 655376 | tf_op jit(solution)/shard_map/reduce_scatter | solution.py:94
  289.4 2.4 copy.52
  291.8 2.5 fusion.59
  294.2 2.5 copy.63
  296.8 2.6 copy.64
  299.4 3.8 subtract_convert_fusion
  303.1 4.6 fusion.60
  307.8 2.0 divide_convert_fusion
  309.7 2.1 copy.58
  311.9 4.8 %all-to-all-start.2 = ((bf16[10,256,256]{2,0,1:T(8,128)(2,1)}), bf16[10,256,256]{2,0,1:T(8,128)(2,1)}, u32[]{:S(2)}, u32[]{:S(2)}) async-start(bf16[10,256,256]{2,0,1:T(8,128)(2,1)} %copy.58), calls=%async_computation.4 | async-start | bytes 4194304 | tf_op jit(solution)/shard_map/all_to_all | solution.py:109
  316.7 16.7 %fusion.40 = f32[16384,128]{1,0:T(8,128)} fusion(bf16[960,16384]{1,0:T(8,128)(2,1)} %bitcast.38, bf16[1000,128]{1,0:T(8,128)(2,1)S(1)} %copy-done.4), kind=kOutput, calls=%fused_computation.42 | convolution fusion | flops 4026531840 | bytes 40091648 | tf_op jit(solution)/shard_map/dot_general | solution.py:115
  333.4 8.8 %all-to-all-done.2 = bf16[10,256,256]{2,0,1:T(8,128)(2,1)} async-done(((bf16[10,256,256]{2,0,1:T(8,128)(2,1)}), bf16[10,256,256]{2,0,1:T(8,128)(2,1)}, u32[]{:S(2)}, u32[]{:S(2)}) %all-to-all-start.2) | async-done | bytes 1310752 | tf_op jit(solution)/shard_map/all_to_all | solution.py:109
  342.2 2.1 copy.59
  344.3 0.8 copy.69
  345.1 6.8 %fusion.65 = (f32[16384]{0:T(1024)S(1)}, f32[16384,128]{1,0:T(8,128)S(1)}) fusion(f32[128]{0:T(128)S(1)} %copy-done.5, f32[16384,128]{1,0:T(8,128)} %fusion.40, bf16[40,16384]{1,0:T(8,128)(2,1)S(1)} %bitcast.42, bf16[1000,128]{1,0:T(8,128)(2,1)S(1)} %copy-done.4), kind=kOutput, calls=%fused_computation.69 | convolution fusion | flops 178241536 | bytes 18164224 | tf_op jit(solution)/shard_map/dot_general | solution.py:116
  352.0 4.9 %multiply_reduce_fusion = f32[16384]{0:T(1024)S(1)} fusion(f32[16384,128]{1,0:T(8,128)S(1)} %get-tuple-element.24, f32[16384]{0:T(1024)S(1)} %broadcast_multiply_fusion), kind=kLoop, calls=%fused_computation.11 | loop fusion | flops 6275072 | bytes 8519680 | tf_op jit(solution)/shard_map/reduce_sum | solution.py:51
  357.0 14.4 %fusion.4 = bf16[16384,128]{1,0:T(8,128)(2,1)} fusion(f32[16384,128]{1,0:T(8,128)} %copy-done.2, bf16[512,128]{1,0:T(8,128)(2,1)S(1)} %copy-done.10, bf16[128,512]{1,0:T(8,128)(2,1)S(1)} %copy-done.11, f32[512]{0:T(512)S(1)} %copy-done.12, f32[128]{0:T(128)S(1)} %copy-done.14, f32[128]{0:T(128)S(1)} %copy-done.15, f32[128]{0:T(128)S(1)} %copy-done.16, ...), kind=kOutput, calls=%fused_computation.7 | convolution fusion | flops 4339007488 | bytes 13045248 | tf_op jit(solution)/shard_map/dot_general | solution.py:56
  371.4 3.7 fusion.17
  375.1 0.5 copy.61
  375.7 97.1 %all_to_all.43 = bf16[8,2048,128]{2,1,0:T(8,128)(2,1)S(1)} all-to-all(bf16[8,2048,128]{2,1,0:T(8,128)(2,1)S(1)} %copy.61), channel_id=1, replica_groups=mesh['dp'=8,'col'=4] {'dp'}, dimensions={0} | all-to-all | bytes 8388608 | tf_op jit(solution)/shard_map/all_to_all | solution.py:146
  472.8 2.0 copy.75
  474.8 0.6 copy-done.1
  (40 shorter events, 0.2 us)
Async XLA Ops:
  6.5 67.5 %copy-start = (bf16[640,1280]{1,0:T(8,128)(2,1)S(1)}, bf16[640,1280]{1,0:T(8,128)(2,1)}, u32[]{:S(2)}) copy-start(bf16[640,1280]{1,0:T(8,128)(2,1)} %param.17) | copy-start | bytes 4915204
  6.5 63.9 %all-gather.2.cloned.1.call-start = ((), (), s32[]{:S(2)}) async-start(), calls=%async_computation.6 | async-start | bytes 3276800 | tf_op jit(solution)/shard_map/all_gather | solution.py:88
  46.8 136.4 %reduce-scatter.5.cloned.1.call-start = ((), (), s32[]{:S(2)}) async-start(), calls=%async_computation.8 | async-start | bytes 5898240 | tf_op jit(solution)/shard_map/reduce_scatter | solution.py:94
  72.5 1.5 copy-start.3
  79.9 1.4 copy-start.9
  80.0 209.4 %reduce-scatter.3.cloned.1.call-start = ((), (), s32[]{:S(2)}) async-start(), calls=%async_computation.7 | async-start | bytes 5898240 | tf_op jit(solution)/shard_map/reduce_scatter | solution.py:94
  89.7 29.3 %copy-start.8 = (s32[1,8]{1,0:T(1,128)S(1)}, s32[1,8]{1,0:T(1,128)}, u32[]{:S(2)}) copy-start(s32[1,8]{1,0:T(1,128)} %param.28) | copy-start | bytes 100
  89.7 29.3 %copy-start.13 = (s32[1,8]{1,0:T(1,128)S(1)}, s32[1,8]{1,0:T(1,128)}, u32[]{:S(2)}) copy-start(s32[1,8]{1,0:T(1,128)} %param.29) | copy-start | bytes 100
  89.7 29.3 %copy-start.7 = (s32[1,8]{1,0:T(1,128)S(1)}, s32[1,8]{1,0:T(1,128)}, u32[]{:S(2)}) copy-start(s32[1,8]{1,0:T(1,128)} %param.30) | copy-start | bytes 100
  311.9 4.9 %copy-start.4 = (bf16[1000,128]{1,0:T(8,128)(2,1)S(1)}, bf16[1000,128]{1,0:T(8,128)(2,1)}, u32[]{:S(2)}) copy-start(bf16[1000,128]{1,0:T(8,128)(2,1)} %param.20) | copy-start | bytes 768004
  311.9 30.4 %all-to-all-start.2 = ((bf16[10,256,256]{2,0,1:T(8,128)(2,1)}), bf16[10,256,256]{2,0,1:T(8,128)(2,1)}, u32[]{:S(2)}, u32[]{:S(2)}) async-start(bf16[10,256,256]{2,0,1:T(8,128)(2,1)} %copy.58), calls=%async_computation.4 | async-start | bytes 4194304 | tf_op jit(solution)/shard_map/all_to_all | solution.py:109
  342.2 2.8 copy-start.5
  351.9 5.0 %copy-start.2 = (f32[16384,128]{1,0:T(8,128)}, f32[16384,128]{1,0:T(8,128)S(1)}, u32[]{:S(2)}) copy-start(f32[16384,128]{1,0:T(8,128)S(1)} %get-tuple-element.24) | copy-start | bytes 25165828
  351.9 5.0 %copy-start.10 = (bf16[512,128]{1,0:T(8,128)(2,1)S(1)}, bf16[512,128]{1,0:T(8,128)(2,1)}, u32[]{:S(2)}) copy-start(bf16[512,128]{1,0:T(8,128)(2,1)} %param.26) | copy-start | bytes 393220
  351.9 5.0 %copy-start.11 = (bf16[128,512]{1,0:T(8,128)(2,1)S(1)}, bf16[128,512]{1,0:T(8,128)(2,1)}, u32[]{:S(2)}) copy-start(bf16[128,512]{1,0:T(8,128)(2,1)} %param.24) | copy-start | bytes 393220
  352.0 5.0 %copy-start.12 = (f32[512]{0:T(512)S(1)}, f32[512]{0:T(512)}, u32[]{:S(2)}) copy-start(f32[512]{0:T(512)} %param.25) | copy-start | bytes 6148
  352.0 5.0 %copy-start.14 = (f32[128]{0:T(128)S(1)}, f32[128]{0:T(128)}, u32[]{:S(2)}) copy-start(f32[128]{0:T(128)} %param.27) | copy-start | bytes 1540
  352.0 5.0 %copy-start.15 = (f32[128]{0:T(128)S(1)}, f32[128]{0:T(128)}, u32[]{:S(2)}) copy-start(f32[128]{0:T(128)} %param.23) | copy-start | bytes 1540
  352.0 5.0 %copy-start.16 = (f32[128]{0:T(128)S(1)}, f32[128]{0:T(128)}, u32[]{:S(2)}) copy-start(f32[128]{0:T(128)} %param.22) | copy-start | bytes 1540
  357.0 14.4 %copy-start.6 = (s32[1,1,8]{2,1,0:T(1,128)S(1)}, s32[1,1,8]{2,1,0:T(1,128)}, u32[]{:S(2)}) copy-start(s32[1,1,8]{2,1,0:T(1,128)} %param.31) | copy-start | bytes 100
  472.8 2.6 copy-start.1
Sparse Core Ops, SparseCore 0:
  46.9 23.5 all-gather.1
  80.1 102.9 reduce-scatter.4
  186.7 102.6 reduce-scatter.2
